TPU v7x, 32 devices: a whole 2x2x4 slice. The times are simulated.
32 devices in a mesh: tile: 8 (over z, x), conv: 4 (over y, core).
Axes of the slice: x: 2, y: 2, z: 4, core: 2. Of those that a mesh axis runs over, the one named last changes fastest.
Arguments:
- field: float32 [256, 24576], P(None, ('tile', 'conv')), may hold values from -6 to 6
- interp: bfloat16 [32768, 384], P(('tile', 'conv')), may hold values from -0.1875 to 0.1875
- conv_blocks: bfloat16 [64, 3, 256, 256], P(('tile', 'conv')), may hold values from -0.21875 to 0.21875
- band_shift: int32 [64, 3], P(('tile', 'conv')), may hold values from 0 to 1
- owner: int32 [12288, 1], P(('tile', 'conv')), may hold values from 0 to 3; in each aligned block of 384 rows (0 to 383, 384 to 767, ...) at most 128 rows name the same one
- edge_index: int32 [64, 128], P(('tile', 'conv')), may hold values from 0 to 767, as said below
Outputs:
- correlated: float32 [256, 24576], P(None, ('tile', 'conv'))
Inputs may be any that keep to these rules, and one draw needn't show every extreme that they name: `edge_index`: row 2b lists the first 128 columns of domain b in some order, row 2b + 1 its last 128 columns in some order. Among the 384 points of one domain no owner is named more than 128 times, and in some domains one owner is named exactly 128 times.
All inputs are finite; a program needn't handle non-finite values.
Results may differ from a plain program's by a relative error of at most 0.0049.
Values may be sent and summed in bfloat16 or wider, within the bound.
A program may use at most 64 MiB of HBM per device.

v0:
```python
import jax
import jax.numpy as jnp
from jax import lax
from jax.sharding import PartitionSpec as P


def padded(cells, sides, width):
    for axis, dim in sides:
        count = lax.axis_size(axis)
        head = lax.slice_in_dim(cells, 0, width, axis=dim)
        tail = lax.slice_in_dim(cells, cells.shape[dim] - width, cells.shape[dim], axis=dim)
        cells = jnp.concatenate(
            [
                lax.ppermute(tail, axis, [(i, (i + 1) % count) for i in range(count)]),
                cells,
                lax.ppermute(head, axis, [((i + 1) % count, i) for i in range(count)]),
            ],
            axis=dim,
        )
    return cells


def contract_last(left_side, right_side):
    return lax.dot_general(
        left_side, right_side, (((1,), (1,)), ((), ())), preferred_element_type=jnp.float32
    )


def convolve(values, conv_blocks, band_shift):
    height = values.shape[0]
    owned_blocks = conv_blocks.shape[0]
    points = conv_blocks.shape[2]
    pieces = values.reshape(height, owned_blocks, points)
    source = (jnp.arange(owned_blocks, dtype=jnp.int32)[:, None] + band_shift) % owned_blocks
    select = (
        source[:, :, None] == jnp.arange(owned_blocks, dtype=jnp.int32)[None, None, :]
    ).astype(jnp.bfloat16)
    picked = jnp.einsum("rsp,jbs->rjbp", pieces, select, preferred_element_type=jnp.float32).astype(
        jnp.bfloat16
    )
    forward = jnp.einsum(
        "rjbp,jbpq->rjq", picked, conv_blocks, preferred_element_type=jnp.float32
    ).astype(jnp.bfloat16)
    backward = jnp.einsum(
        "rjq,jbpq->rjbp", forward, conv_blocks, preferred_element_type=jnp.float32
    )
    adjoint = jnp.einsum(
        "rjbp,jbs->rsp", backward, select.astype(jnp.float32), precision=lax.Precision.HIGHEST
    )
    return adjoint.reshape(height, owned_blocks * points).astype(jnp.bfloat16)


def on_device(field, interp, conv_blocks, band_shift, owner, edge_index):
    columns = field.shape[1]
    rim_width = edge_index.shape[1]
    groups = lax.axis_size("conv")
    slot_count = conv_blocks.shape[0] * conv_blocks.shape[2]
    capacity = slot_count // groups
    rounded = field.astype(jnp.bfloat16)
    left_list = edge_index[0]
    right_list = edge_index[1]
    rim_values = jnp.concatenate(
        [jnp.take(rounded, left_list, axis=1), jnp.take(rounded, right_list, axis=1)], axis=1
    )
    widened = padded(rim_values, ((("tile", "conv"), 1),), rim_width)
    from_left = widened[:, :rim_width]
    from_right = widened[:, 3 * rim_width :]
    extended = jnp.concatenate([from_left, rounded, from_right], axis=1)
    subgrid = jnp.dot(extended, interp, preferred_element_type=jnp.float32)
    subgrid = subgrid.astype(jnp.bfloat16)
    owners = owner[:, 0]
    choose = (owners[:, None] == jnp.arange(groups, dtype=jnp.int32)[None, :]).astype(jnp.int32)
    before = jnp.cumsum(choose, axis=0) - choose
    position = jnp.sum(before * choose, axis=1)
    slot_index = owners * capacity + position
    placement = (slot_index[:, None] == jnp.arange(slot_count, dtype=jnp.int32)[None, :]).astype(
        jnp.bfloat16
    )
    outgoing = jnp.dot(subgrid, placement, preferred_element_type=jnp.float32).astype(jnp.bfloat16)
    incoming = lax.all_to_all(
        convolve(
            lax.all_to_all(outgoing, "conv", split_axis=1, concat_axis=1, tiled=True),
            conv_blocks,
            band_shift,
        ),
        "conv",
        split_axis=1,
        concat_axis=1,
        tiled=True,
    )
    returned = contract_last(incoming, placement).astype(jnp.bfloat16)
    partial_value = contract_last(returned, interp)
    left_part = partial_value[:, :rim_width]
    right_part = partial_value[:, rim_width + columns :]
    edge_sums = padded(
        jnp.concatenate([left_part, right_part], axis=1).astype(jnp.bfloat16),
        ((("tile", "conv"), 1),),
        rim_width,
    ).astype(jnp.float32)
    interior_part = partial_value[:, rim_width : rim_width + columns]
    result = interior_part.at[:, left_list].add(edge_sums[:, :rim_width])
    result = result.at[:, right_list].add(edge_sums[:, 3 * rim_width :])
    return result


def solution(mesh):
    return jax.shard_map(
        on_device,
        mesh=mesh,
        in_specs=(
            P(None, ("tile", "conv")),
            P(("tile", "conv"), None),
            P(("tile", "conv"), None, None, None),
            P(("tile", "conv"), None),
            P(("tile", "conv"), None),
            P(("tile", "conv"), None),
        ),
        out_specs=P(None, ("tile", "conv")),
        check_vma=False,
    )
```

profile of v0, /device:TPU:0, one launch (start us, length us, event | category | flops | bytes accessed | tf_op | source)
XLA Modules:
  0.0 51.1 jit_solution(18035988229664410516)
XLA Ops:
  0.0 0.0 copy-start
  0.0 0.0 copy-start.1
  0.0 0.8 %compare_and_fusion.1 = (pred[128]{0:T(512)(128)(4,1)S(1)}, s32[128]{0:T(128)S(1)}, pred[128]{0:T(512)(128)(4,1)S(1)}, s32[128]{0:T(128)S(1)}) fusion(s32[2,128]{1,0:T(2,128)} %param.13), kind=kLoop, calls=%fused_computation.58 | loop fusion | flops 1536 | bytes 2304 | tf_op jit(solution)/shard_map/jit(_take)/and | solution.py:63
  0.8 1.3 %copy.27 = bf16[256,768]{0,1:T(8,128)(2,1)S(1)} copy(f32[256,768]{1,0:T(8,128)} %param.8) | data formatting | bytes 1179648 | tf_op args[0]
  2.1 0.8 %gather_fusion = bf16[128,256]{1,0:T(8,128)(2,1)S(1)} fusion(bf16[256,768]{0,1:T(8,128)(2,1)S(1)} %copy.27, s32[1024]{0:T(1024)S(1)} %pad_clamp_fusion.1), kind=kCustom, calls=%fused_computation.clone | custom fusion | bytes 131584 | tf_op jit(solution)/shard_map/jit(_take)/gather | solution.py:63
  3.0 0.1 select_bitcast_fusion.1
  3.1 0.5 %collective-permute-start = (bf16[256,128]{0,1:T(8,128)(2,1)S(1)}, bf16[256,128]{0,1:T(8,128)(2,1)S(1)}, u32[]{:S(2)}, u32[]{:S(2)}) collective-permute-start(bf16[256,128]{0,1:T(8,128)(2,1)S(1)} %select_bitcast_fusion.1), channel_id=1, source_target_pairs={{0,1},{1,2},{2,3},{3,4},{4,5},{5,6},{6,7},{7,8},{8,9},{9,10},{10,1... | collective-permute-start | bytes 196616 | tf_op jit(solution)/shard_map/ppermute | solution.py:14
  3.6 0.8 %gather_fusion.1 = bf16[128,256]{1,0:T(8,128)(2,1)S(1)} fusion(bf16[256,768]{0,1:T(8,128)(2,1)S(1)} %copy.27, s32[1024]{0:T(1024)S(1)} %pad_clamp_fusion), kind=kCustom, calls=%fused_computation.1.clone | custom fusion | bytes 131584 | tf_op jit(solution)/shard_map/jit(_take)/gather | solution.py:63
  4.5 0.1 select_bitcast_fusion
  4.5 6.0 %collective-permute-start.1 = (bf16[256,128]{0,1:T(8,128)(2,1)S(1)}, bf16[256,128]{0,1:T(8,128)(2,1)S(1)}, u32[]{:S(2)}, u32[]{:S(2)}) collective-permute-start(bf16[256,128]{0,1:T(8,128)(2,1)S(1)} %select_bitcast_fusion), channel_id=1, source_target_pairs={{1,0},{2,1},{3,2},{4,3},{5,4},{6,5},{7,6},{8,7},{9,8},{10,9},{11,1... | collective-permute-start | bytes 196616 | tf_op jit(solution)/shard_map/ppermute | solution.py:16
  10.5 0.0 copy-done.1
  10.6 1.2 %reduce-window.6 = s32[4,3,128]{2,1,0:T(4,128)S(1)} reduce-window(s32[4,3,128]{2,1,0:T(4,128)S(1)} %fusion.32, s32[]{:T(128)} %constant.30.clone.1), window={size=1x1x128 pad=0_0x0_0x127_0}, to_apply=%region_0.0 | reduce-window | flops 195072 | bytes 12292 | tf_op jit(solution)/shard_map/reduce-window
  11.8 0.2 slice_reduce_fusion
  12.0 0.2 reduce-window.9
  12.2 0.1 add_bitcast_fusion
  12.3 0.0 copy-start.3
  12.3 0.0 collective-permute-done
  12.3 0.1 collective-permute-done.1
  12.4 0.0 copy-done
  12.4 0.7 %fusion.10 = bf16[32,4,8,128]{3,2,1,0:T(8,128)(2,1)S(1)} fusion(bf16[1024,384]{1,0:T(8,128)(2,1)S(1)} %copy-done, bf16[256,128]{0,1:T(8,128)(2,1)S(1)} %collective-permute-done.1, bf16[256,768]{0,1:T(8,128)(2,1)S(1)} %copy.27, bf16[256,128]{0,1:T(8,128)(2,1)S(1)} %collective-permute-done, s32[384]{0:T(512)S(1)} %add_reduce_fusion), kind=kOutput, calls=%fused_computation.16 | convolution fusion | flops 303988736 | bytes 1574400 | tf_op jit(solution)/shard_map/dot_general | solution.py:79
  13.1 0.7 %copy.58 = bf16[32,4,8,128]{3,2,0,1:T(8,128)(2,1)} copy(bf16[32,4,8,128]{3,2,1,0:T(8,128)(2,1)S(1)} %fusion.10) | data formatting | bytes 524288 | tf_op jit(solution)/shard_map/all_to_all | solution.py:82
  13.9 3.4 %all-to-all-start = ((bf16[256,4,128]{2,0,1:T(8,128)(2,1)}), bf16[256,4,128]{2,0,1:T(8,128)(2,1)S(1)}, u32[]{:S(2)}, u32[]{:S(2)}) async-start(bf16[256,4,128]{2,0,1:T(8,128)(2,1)} %bitcast.89), calls=%async_computation | async-start | bytes 524288 | tf_op jit(solution)/shard_map/all_to_all | solution.py:82
  17.3 0.0 copy-done.3
  17.3 5.9 %all-to-all-done = bf16[256,4,128]{2,0,1:T(8,128)(2,1)S(1)} async-done(((bf16[256,4,128]{2,0,1:T(8,128)(2,1)}), bf16[256,4,128]{2,0,1:T(8,128)(2,1)S(1)}, u32[]{:S(2)}, u32[]{:S(2)}) %all-to-all-start) | async-done | bytes 262176 | tf_op jit(solution)/shard_map/all_to_all | solution.py:82
  23.3 0.2 copy.29
  23.5 0.2 reshape.131
  23.7 1.0 %fusion.2 = bf16[256,2,3,256]{3,2,0,1:T(4,128)(2,1)S(1)} fusion(bf16[256,2,256,1]{2,1,0,3:T(2,128)(2,1)S(1)} %reshape.131, s32[2,3]{1,0:T(2,128)S(1)} %and_select_fusion), kind=kOutput, calls=%fused_computation.8 | convolution fusion | flops 1966092 | bytes 1048600 | tf_op jit(solution)/shard_map/rsp,jbs->rjbp/dot_general | solution.py:38
  24.7 2.0 %convolution_bitcast_fusion = f32[256,2,3,256]{3,0,2,1:T(8,128)S(1)} fusion(bf16[2,3,256,256]{3,2,1,0:T(8,128)(2,1)} %param.10, bf16[256,2,3,256]{3,2,0,1:T(4,128)(2,1)S(1)} %fusion.2), kind=kOutput, calls=%fused_computation.6 | convolution fusion | flops 402784256 | bytes 3145728 | tf_op jit(solution)/shard_map/rjq,jbpq->rjbp/dot_general | solution.py:44
  26.7 2.9 %fusion.11 = bf16[256,2,256]{2,1,0:T(2,128)(2,1)S(1)} fusion(f32[256,2,3,256]{3,0,2,1:T(8,128)S(1)} %convolution_bitcast_fusion, s32[2,3]{1,0:T(2,128)S(1)} %and_select_fusion), kind=kOutput, calls=%fused_computation.17 | convolution fusion | flops 9568268 | bytes 1835032 | tf_op jit(solution)/shard_map/rjbp,jbs->rsp/dot_general | solution.py:47
  29.6 0.2 convert_element_type.59
  29.9 8.4 %all_to_all.18 = bf16[256,4,128]{2,0,1:T(8,128)(2,1)S(1)} all-to-all(bf16[256,4,128]{2,0,1:T(8,128)(2,1)S(1)} %copy.32), channel_id=1, replica_groups=mesh['tile'=8,'conv'=4] {'conv'}, dimensions={1} | all-to-all | bytes 524288 | tf_op jit(solution)/shard_map/all_to_all | solution.py:80
  38.3 0.1 copy.33
  38.4 0.0 copy-start.2
  38.4 0.8 %fusion.46 = (bf16[256,1024]{1,0:T(8,128)(2,1)S(1)}, f32[256,1024]{1,0:T(8,128)S(1)}) fusion(bf16[1024,384]{1,0:T(8,128)(2,1)S(1)} %copy-done, bf16[256,512]{0,1:T(8,128)(2,1)S(1)} %bitcast.91, s32[384]{0:T(512)S(1)} %add_reduce_fusion), kind=kOutput, calls=%fused_computation.68 | convolution fusion | flops 302546944 | bytes 2622976 | tf_op jit(solution)/shard_map/dot_general | solution.py:24
  39.2 0.1 collective-permute-start.2
  39.3 5.3 %collective-permute-start.3 = (bf16[256,128]{1,0:T(8,128)(2,1)S(1)}, bf16[256,128]{1,0:T(8,128)(2,1)S(1)}, u32[]{:S(2)}, u32[]{:S(2)}) collective-permute-start(bf16[256,128]{1,0:T(8,128)(2,1)S(1)} %get-tuple-element.11), channel_id=1, source_target_pairs={{1,0},{2,1},{3,2},{4,3},{5,4},{6,5},{7,6},{8,7},{9,8},{10,9},{11,1... | collective-permute-start | bytes 196616 | tf_op jit(solution)/shard_map/ppermute | solution.py:16
  44.6 0.0 copy-done.2
  44.6 0.1 slice.45
  44.7 0.3 copy.34
  45.0 1.6 %collective-permute-done.2 = bf16[256,128]{1,0:T(8,128)(2,1)S(1)} collective-permute-done((bf16[256,128]{1,0:T(8,128)(2,1)S(1)}, bf16[256,128]{1,0:T(8,128)(2,1)S(1)}, u32[]{:S(2)}, u32[]{:S(2)}) %collective-permute-start.2) | collective-permute-done | bytes 65568 | tf_op jit(solution)/shard_map/ppermute | solution.py:14
  46.6 0.0 collective-permute-done.3
  46.6 0.1 copy.35
  46.7 0.1 copy.36
  46.8 1.6 %scatter_fusion = f32[256,768]{0,1:T(8,128)S(1)} fusion(f32[256,768]{0,1:T(8,128)S(1)} %copy.34, s32[128]{0:T(128)S(1)} %get-tuple-element.15, f32[128,256]{1,0:T(8,128)S(1)} %copy.35), kind=kCustom, calls=%fused_computation.2 | custom fusion | flops 32768 | bytes 393728 | tf_op jit(solution)/shard_map/scatter-add | solution.py:101
  48.4 1.6 %scatter_fusion.1 = f32[256,768]{0,1:T(8,128)S(1)} fusion(f32[256,768]{0,1:T(8,128)S(1)} %scatter_fusion, s32[128]{0:T(128)S(1)} %get-tuple-element.14, f32[128,256]{1,0:T(8,128)S(1)} %copy.36), kind=kCustom, calls=%fused_computation.3 | custom fusion | flops 32768 | bytes 393728 | tf_op jit(solution)/shard_map/scatter-add | solution.py:102
  50.0 1.1 %copy.37 = f32[256,768]{1,0:T(8,128)} copy(f32[256,768]{0,1:T(8,128)S(1)} %scatter_fusion.1) | data formatting | bytes 1572864 | tf_op jit(solution)/shard_map/scatter-add | solution.py:102
  (11 shorter events, 0.2 us)
Async XLA Ops:
  0.0 12.4 %copy-start = (bf16[1024,384]{1,0:T(8,128)(2,1)S(1)}, bf16[1024,384]{1,0:T(8,128)(2,1)}, u32[]{:S(2)}) copy-start(bf16[1024,384]{1,0:T(8,128)(2,1)} %param.9) | copy-start | bytes 2359300
  0.0 10.5 %copy-start.1 = (s32[384,1]{0,1:T(1,128)S(1)}, s32[384,1]{0,1:T(1,128)}, u32[]{:S(2)}) copy-start(s32[384,1]{0,1:T(1,128)} %param.12) | copy-start | bytes 4612
  3.1 9.3 %collective-permute-start = (bf16[256,128]{0,1:T(8,128)(2,1)S(1)}, bf16[256,128]{0,1:T(8,128)(2,1)S(1)}, u32[]{:S(2)}, u32[]{:S(2)}) collective-permute-start(bf16[256,128]{0,1:T(8,128)(2,1)S(1)} %select_bitcast_fusion.1), channel_id=1, source_target_pairs={{0,1},{1,2},{2,3},{3,4},{4,5},{5,6},{6,7},{7,8},{8,9},{9,10},{10,1... | collective-permute-start | bytes 196616 | tf_op jit(solution)/shard_map/ppermute | solution.py:14
  4.5 7.9 %collective-permute-start.1 = (bf16[256,128]{0,1:T(8,128)(2,1)S(1)}, bf16[256,128]{0,1:T(8,128)(2,1)S(1)}, u32[]{:S(2)}, u32[]{:S(2)}) collective-permute-start(bf16[256,128]{0,1:T(8,128)(2,1)S(1)} %select_bitcast_fusion), channel_id=1, source_target_pairs={{1,0},{2,1},{3,2},{4,3},{5,4},{6,5},{7,6},{8,7},{9,8},{10,9},{11,1... | collective-permute-start | bytes 196616 | tf_op jit(solution)/shard_map/ppermute | solution.py:16
  12.3 5.0 %copy-start.3 = (s32[2,3]{1,0:T(2,128)S(1)}, s32[2,3]{1,0:T(2,128)}, u32[]{:S(2)}) copy-start(s32[2,3]{1,0:T(2,128)} %param.11) | copy-start | bytes 76
  13.9 9.4 %all-to-all-start = ((bf16[256,4,128]{2,0,1:T(8,128)(2,1)}), bf16[256,4,128]{2,0,1:T(8,128)(2,1)S(1)}, u32[]{:S(2)}, u32[]{:S(2)}) async-start(bf16[256,4,128]{2,0,1:T(8,128)(2,1)} %bitcast.89), calls=%async_computation | async-start | bytes 524288 | tf_op jit(solution)/shard_map/all_to_all | solution.py:82
  38.4 6.2 %copy-start.2 = (s32[2,128]{1,0:T(2,128)S(1)}, s32[2,128]{1,0:T(2,128)}, u32[]{:S(2)}) copy-start(s32[2,128]{1,0:T(2,128)} %param.13) | copy-start | bytes 3076
  39.2 7.3 %collective-permute-start.2 = (bf16[256,128]{1,0:T(8,128)(2,1)S(1)}, bf16[256,128]{1,0:T(8,128)(2,1)S(1)}, u32[]{:S(2)}, u32[]{:S(2)}) collective-permute-start(bf16[256,128]{1,0:T(8,128)(2,1)S(1)} %get-tuple-element.10), channel_id=1, source_target_pairs={{0,1},{1,2},{2,3},{3,4},{4,5},{5,6},{6,7},{7,8},{8,9},{9,10},{10,1... | collective-permute-start | bytes 196616 | tf_op jit(solution)/shard_map/ppermute | solution.py:14
  39.3 7.3 %collective-permute-start.3 = (bf16[256,128]{1,0:T(8,128)(2,1)S(1)}, bf16[256,128]{1,0:T(8,128)(2,1)S(1)}, u32[]{:S(2)}, u32[]{:S(2)}) collective-permute-start(bf16[256,128]{1,0:T(8,128)(2,1)S(1)} %get-tuple-element.11), channel_id=1, source_target_pairs={{1,0},{2,1},{3,2},{4,3},{5,4},{6,5},{7,6},{8,7},{9,8},{10,9},{11,1... | collective-permute-start | bytes 196616 | tf_op jit(solution)/shard_map/ppermute | solution.py:16
where the time goes:
time: 51.4 us; the launch traced here: 51.1 us
  starting transfers between devices  15.3 us (30%)
  blocking collectives  8.39 us (16%)
  waiting for transfers between devices  7.66 us (15%)
  matrix products  7.43 us (14%)
  local copies, waits for them, and re-layouts  6.38 us (12%)
  other arithmetic  5.73 us (11%)
    ppermute x2, starting transfers between devices, padded(): lax.ppermute(head, axis, [((i + 1) % count, i) for i in range(count)])  11.3 us
    all_to_all x1, blocking collectives, on_device(): lax.all_to_all(convolve(lax.all_to_all(outgoing, 'conv', split_axis=1, co...  8.39 us
    all_to_all x1, waiting for transfers between devices, on_device(): lax.all_to_all(outgoing, 'conv', split_axis=1, concat_axis=1, tiled=True)  5.95 us
    all_to_all x1, starting transfers between devices, on_device(): lax.all_to_all(outgoing, 'conv', split_axis=1, concat_axis=1, tiled=True)  3.41 us
    dot_general x1, matrix products, convolve(): jnp.einsum('rjbp,jbs->rsp', backward, select.astype(jnp.float32), precisi...  2.94 us
    dot_general x1, matrix products, convolve(): jnp.einsum('rjq,jbpq->rjbp', forward, conv_blocks, preferred_element_type...  2.02 us
    ppermute x2, waiting for transfers between devices, padded(): lax.ppermute(tail, axis, [(i, (i + 1) % count) for i in range(count)])  1.61 us
    scatter-add x1, other arithmetic, on_device(): result = interior_part.at[:, left_list].add(edge_sums[:, :rim_width])  1.59 us
  transfers between devices with their start and end apart: 5, of which 3 were waited for; matrix products, arithmetic and copies ran while one was open for 6% of the time, Pallas kernels for 0%

commit v1 on v0

--- a/solution.py
+++ b/solution.py
@@ -2,6 +2,29 @@
 import jax.numpy as jnp
 from jax import lax
 from jax.sharding import PartitionSpec as P
+
+
+def cut_along(value, dim, peers):
+    shape = value.shape
+    blocks = value.reshape(*shape[:dim], peers, shape[dim] // peers, *shape[dim + 1 :])
+    return jnp.moveaxis(blocks, dim, 0)
+
+
+def in_order(blocks, dim):
+    blocks = jnp.moveaxis(blocks, 0, dim)
+    shape = blocks.shape
+    return blocks.reshape(*shape[:dim], shape[dim] * shape[dim + 1], *shape[dim + 2 :])
+
+
+def swapped_with_each(x, axis, split_dim, concat_dim):
+    devices, index = (lax.axis_size(axis), lax.axis_index(axis))
+    parts = cut_along(x, split_dim, devices)
+    done = [parts[index]]
+    for lap in range(1, devices):
+        sent = parts[index ^ lap]
+        done.append(lax.ppermute(sent, axis, [(i, i ^ lap) for i in range(devices)]))
+    parts = jnp.stack(done)[index ^ jnp.arange(devices)]
+    return in_order(parts, concat_dim)
 
 
 def padded(cells, sides, width):
@@ -77,16 +100,15 @@
         jnp.bfloat16
     )
     outgoing = jnp.dot(subgrid, placement, preferred_element_type=jnp.float32).astype(jnp.bfloat16)
-    incoming = lax.all_to_all(
+    incoming = swapped_with_each(
         convolve(
             lax.all_to_all(outgoing, "conv", split_axis=1, concat_axis=1, tiled=True),
             conv_blocks,
             band_shift,
         ),
         "conv",
-        split_axis=1,
-        concat_axis=1,
-        tiled=True,
+        1,
+        1,
     )
     returned = contract_last(incoming, placement).astype(jnp.bfloat16)
     partial_value = contract_last(returned, interp)

time: 51.4 us -> 49.8 us (0.969)
  blocking collectives: 8.39 us -> 0 us
  waiting for transfers between devices: 7.66 us -> 11.1 us
  starting transfers between devices: 15.3 us -> 17.4 us
  local copies, waits for them, and re-layouts: 6.38 us -> 7.54 us
    all_to_all x1 -> x0, blocking collectives: 8.39 us -> none  [on_device(): lax.all_to_all(convolve(lax.all_to_all(outgoing, 'conv', split_axis=1, co...]
    ppermute x0 -> x3, waiting for transfers between devices: none -> 3.46 us  [swapped_with_each(): lax.ppermute(sent, axis, [(i, i ^ lap) for i in range(devices)])]
    ppermute x0 -> x3, starting transfers between devices: none -> 2.04 us  [swapped_with_each(): lax.ppermute(sent, axis, [(i, i ^ lap) for i in range(devices)])]
    gather x0 -> x1, local copies, waits for them, and re-layouts: none -> 0.6 us  [swapped_with_each(): parts = jnp.stack(done)[index ^ jnp.arange(devices)]]
    another operation x0 -> x1, local copies, waits for them, and re-layouts: none -> 0.55 us
    unnamed x9 -> x13, local copies, waits for them, and re-layouts: 1.32 us -> 1.37 us
    another operation x2 -> x3, other arithmetic: 1.4 us -> 1.44 us
  transfers between devices with their start and end apart: 5 -> 8, of which waited for: 3 -> 5; matrix products, arithmetic and copies ran while one was open for 6% -> 6% of each run, Pallas kernels for 0% -> 0%
where the time goes in v1:
time: 49.8 us; the launch traced here: 49.5 us
  starting transfers between devices  17.4 us (35%)
  waiting for transfers between devices  11.1 us (22%)
  local copies, waits for them, and re-layouts  7.54 us (15%)
  matrix products  7.44 us (15%)
  other arithmetic  5.78 us (12%)
    ppermute x2, starting transfers between devices, padded(): lax.ppermute(head, axis, [((i + 1) % count, i) for i in range(count)])  11 us
    all_to_all x1, waiting for transfers between devices, on_device(): lax.all_to_all(outgoing, 'conv', split_axis=1, concat_axis=1, tiled=True)  5.95 us
    ppermute x3, waiting for transfers between devices, swapped_with_each(): lax.ppermute(sent, axis, [(i, i ^ lap) for i in range(devices)])  3.46 us
    all_to_all x1, starting transfers between devices, on_device(): lax.all_to_all(outgoing, 'conv', split_axis=1, concat_axis=1, tiled=True)  3.41 us
    dot_general x1, matrix products, convolve(): jnp.einsum('rjbp,jbs->rsp', backward, select.astype(jnp.float32), precisi...  2.94 us
    ppermute x3, starting transfers between devices, swapped_with_each(): lax.ppermute(sent, axis, [(i, i ^ lap) for i in range(devices)])  2.04 us
    dot_general x1, matrix products, convolve(): jnp.einsum('rjq,jbpq->rjbp', forward, conv_blocks, preferred_element_type...  2.02 us
    ppermute x2, waiting for transfers between devices, padded(): lax.ppermute(tail, axis, [(i, (i + 1) % count) for i in range(count)])  1.61 us
  transfers between devices with their start and end apart: 8, of which 5 were waited for; matrix products, arithmetic and copies ran while one was open for 6% of the time, Pallas kernels for 0%

profile of v1, /device:TPU:0, one launch (start us, length us, event | category | flops | bytes accessed | tf_op | source)
XLA Modules:
  0.0 49.5 jit_solution(12062524775466962012)
XLA Ops:
  0.0 0.0 copy-start
  0.0 0.0 copy-start.1
  0.0 0.8 %compare_and_fusion.1 = (pred[128]{0:T(512)(128)(4,1)S(1)}, s32[128]{0:T(128)S(1)}, pred[128]{0:T(512)(128)(4,1)S(1)}, s32[128]{0:T(128)S(1)}) fusion(s32[2,128]{1,0:T(2,128)} %param.13), kind=kLoop, calls=%fused_computation.66 | loop fusion | flops 1536 | bytes 2304 | tf_op jit(solution)/shard_map/jit(_take)/and | solution.py:86
  0.8 1.3 %copy.22 = bf16[256,768]{0,1:T(8,128)(2,1)S(1)} copy(f32[256,768]{1,0:T(8,128)} %param.8) | data formatting | bytes 1179648 | tf_op args[0]
  2.1 0.8 %gather_fusion.1 = bf16[128,256]{1,0:T(8,128)(2,1)S(1)} fusion(bf16[256,768]{0,1:T(8,128)(2,1)S(1)} %copy.22, s32[1024]{0:T(1024)S(1)} %pad_clamp_fusion.2), kind=kCustom, calls=%fused_computation.clone | custom fusion | bytes 131584 | tf_op jit(solution)/shard_map/jit(_take)/gather | solution.py:86
  3.0 0.1 select_bitcast_fusion.1
  3.1 0.5 %collective-permute-start = (bf16[256,128]{0,1:T(8,128)(2,1)S(1)}, bf16[256,128]{0,1:T(8,128)(2,1)S(1)}, u32[]{:S(2)}, u32[]{:S(2)}) collective-permute-start(bf16[256,128]{0,1:T(8,128)(2,1)S(1)} %select_bitcast_fusion.1), channel_id=1, source_target_pairs={{0,1},{1,2},{2,3},{3,4},{4,5},{5,6},{6,7},{7,8},{8,9},{9,10},{10,1... | collective-permute-start | bytes 196616 | tf_op jit(solution)/shard_map/ppermute | solution.py:37
  3.6 0.8 %gather_fusion.2 = bf16[128,256]{1,0:T(8,128)(2,1)S(1)} fusion(bf16[256,768]{0,1:T(8,128)(2,1)S(1)} %copy.22, s32[1024]{0:T(1024)S(1)} %pad_clamp_fusion.1), kind=kCustom, calls=%fused_computation.1.clone | custom fusion | bytes 131584 | tf_op jit(solution)/shard_map/jit(_take)/gather | solution.py:86
  4.5 0.1 select_bitcast_fusion
  4.5 6.0 %collective-permute-start.1 = (bf16[256,128]{0,1:T(8,128)(2,1)S(1)}, bf16[256,128]{0,1:T(8,128)(2,1)S(1)}, u32[]{:S(2)}, u32[]{:S(2)}) collective-permute-start(bf16[256,128]{0,1:T(8,128)(2,1)S(1)} %select_bitcast_fusion), channel_id=1, source_target_pairs={{1,0},{2,1},{3,2},{4,3},{5,4},{6,5},{7,6},{8,7},{9,8},{10,9},{11,1... | collective-permute-start | bytes 196616 | tf_op jit(solution)/shard_map/ppermute | solution.py:39
  10.5 0.0 copy-done.1
  10.6 1.2 %reduce-window.6 = s32[4,3,128]{2,1,0:T(4,128)S(1)} reduce-window(s32[4,3,128]{2,1,0:T(4,128)S(1)} %fusion.32, s32[]{:T(128)} %constant.16.clone.1), window={size=1x1x128 pad=0_0x0_0x127_0}, to_apply=%region_0.0 | reduce-window | flops 195072 | bytes 12292 | tf_op jit(solution)/shard_map/reduce-window
  11.8 0.2 slice_reduce_fusion
  12.0 0.2 reduce-window.9
  12.2 0.1 add_bitcast_fusion
  12.3 0.0 copy-start.3
  12.3 0.0 collective-permute-done
  12.4 0.1 collective-permute-done.1
  12.4 0.0 copy-done
  12.4 0.7 %fusion.10 = bf16[32,4,8,128]{3,2,1,0:T(8,128)(2,1)S(1)} fusion(bf16[1024,384]{1,0:T(8,128)(2,1)S(1)} %copy-done, bf16[256,128]{0,1:T(8,128)(2,1)S(1)} %collective-permute-done.1, bf16[256,768]{0,1:T(8,128)(2,1)S(1)} %copy.22, bf16[256,128]{0,1:T(8,128)(2,1)S(1)} %collective-permute-done, s32[384]{0:T(512)S(1)} %add_reduce_fusion), kind=kOutput, calls=%fused_computation.17 | convolution fusion | flops 303988736 | bytes 1574400 | tf_op jit(solution)/shard_map/dot_general | solution.py:102
  13.1 0.7 %copy.64 = bf16[32,4,8,128]{3,2,0,1:T(8,128)(2,1)} copy(bf16[32,4,8,128]{3,2,1,0:T(8,128)(2,1)S(1)} %fusion.10) | data formatting | bytes 524288 | tf_op jit(solution)/shard_map/all_to_all | solution.py:105
  13.9 3.4 %all-to-all-start = ((bf16[256,4,128]{2,0,1:T(8,128)(2,1)}), bf16[256,4,128]{2,0,1:T(8,128)(2,1)S(1)}, u32[]{:S(2)}, u32[]{:S(2)}) async-start(bf16[256,4,128]{2,0,1:T(8,128)(2,1)} %bitcast.103), calls=%async_computation | async-start | bytes 524288 | tf_op jit(solution)/shard_map/all_to_all | solution.py:105
  17.3 0.0 copy-done.3
  17.3 5.9 %all-to-all-done = bf16[256,4,128]{2,0,1:T(8,128)(2,1)S(1)} async-done(((bf16[256,4,128]{2,0,1:T(8,128)(2,1)}), bf16[256,4,128]{2,0,1:T(8,128)(2,1)S(1)}, u32[]{:S(2)}, u32[]{:S(2)}) %all-to-all-start) | async-done | bytes 262176 | tf_op jit(solution)/shard_map/all_to_all | solution.py:105
  23.3 0.2 copy.24
  23.5 0.2 reshape.165
  23.7 1.0 %fusion.2 = bf16[256,2,3,256]{3,2,0,1:T(4,128)(2,1)S(1)} fusion(bf16[256,2,256,1]{2,1,0,3:T(2,128)(2,1)S(1)} %reshape.165, s32[2,3]{1,0:T(2,128)S(1)} %and_select_fusion), kind=kOutput, calls=%fused_computation.9 | convolution fusion | flops 1966092 | bytes 1048600 | tf_op jit(solution)/shard_map/rsp,jbs->rjbp/dot_general | solution.py:61
  24.7 2.0 %convolution_bitcast_fusion = f32[256,2,3,256]{3,0,2,1:T(8,128)S(1)} fusion(bf16[2,3,256,256]{3,2,1,0:T(8,128)(2,1)} %param.10, bf16[256,2,3,256]{3,2,0,1:T(4,128)(2,1)S(1)} %fusion.2), kind=kOutput, calls=%fused_computation.7 | convolution fusion | flops 402784256 | bytes 3145728 | tf_op jit(solution)/shard_map/rjq,jbpq->rjbp/dot_general | solution.py:67
  26.7 2.9 %fusion.11 = bf16[256,2,256]{2,1,0:T(2,128)(2,1)S(1)} fusion(f32[256,2,3,256]{3,0,2,1:T(8,128)S(1)} %convolution_bitcast_fusion, s32[2,3]{1,0:T(2,128)S(1)} %and_select_fusion), kind=kOutput, calls=%fused_computation.18 | convolution fusion | flops 9568268 | bytes 1835032 | tf_op jit(solution)/shard_map/rjbp,jbs->rsp/dot_general | solution.py:70
  29.6 0.2 convert_element_type.59
  29.8 0.6 %constant_dynamic-slice_fusion.3 = (bf16[256,1,128]{2,1,0:T(2,128)(2,1)S(1)}, bf16[256,1,128]{2,1,0:T(2,128)(2,1)S(1)}, bf16[256,1,128]{2,1,0:T(2,128)(2,1)S(1)}, bf16[256,1,128]{2,1,0:T(2,128)(2,1)S(1)}) fusion(bf16[256,4,128]{2,1,0:T(4,128)(2,1)S(1)} %convert_element_type.59, s32[]{:T(128)S(6)} %select_n.57, s32[]{:T(128)S(6)} %select_n.59, ...), kind=kLoop, calls=%fused_computation.75 | loop fusion | bytes 524304 | tf_op jit(solution)/shard_map/dynamic-slice
  30.4 0.1 collective-permute-start.2
  30.5 0.5 collective-permute-start.3
  31.0 1.5 %collective-permute-start.4 = (bf16[256,128]{1,0:T(8,128)(2,1)S(1)}, bf16[256,128]{1,0:T(8,128)(2,1)S(1)}, u32[]{:S(2)}, u32[]{:S(2)}) collective-permute-start(bf16[256,128]{1,0:T(8,128)(2,1)S(1)} %bitcast.114), channel_id=1, source_target_pairs={{0,3},{1,2},{2,1},{3,0},{4,7},{5,6},{6,5},{7,4},{8,11},{9,10},{10,... | collective-permute-start | bytes 196616 | tf_op jit(solution)/shard_map/ppermute | solution.py:25
  32.5 0.0 collective-permute-done.2
  32.5 3.0 %collective-permute-done.3 = bf16[256,128]{1,0:T(8,128)(2,1)S(1)} collective-permute-done((bf16[256,128]{1,0:T(8,128)(2,1)S(1)}, bf16[256,128]{1,0:T(8,128)(2,1)S(1)}, u32[]{:S(2)}, u32[]{:S(2)}) %collective-permute-start.3) | collective-permute-done | bytes 65568 | tf_op jit(solution)/shard_map/ppermute | solution.py:25
  35.5 0.4 collective-permute-done.4
  36.0 0.6 %gather_fusion = bf16[4,256,128]{2,1,0:T(8,128)(2,1)S(1)} fusion(bf16[4,256,128]{2,1,0:T(8,128)(2,1)S(1)} %pad_maximum_fusion, s32[1024]{0:T(1024)S(1)} %pad_clamp_fusion), kind=kCustom, calls=%fused_computation.2 | custom fusion | bytes 524304 | tf_op jit(solution)/shard_map/gather | solution.py:26
  36.6 0.1 copy.31
  36.8 0.0 copy-start.2
  36.8 0.8 %fusion.47 = (bf16[256,1024]{1,0:T(8,128)(2,1)S(1)}, f32[256,1024]{1,0:T(8,128)S(1)}) fusion(bf16[1024,384]{1,0:T(8,128)(2,1)S(1)} %copy-done, bf16[256,512]{0,1:T(8,128)(2,1)S(1)} %bitcast.109, s32[384]{0:T(512)S(1)} %add_reduce_fusion), kind=kOutput, calls=%fused_computation.81 | convolution fusion | flops 302546944 | bytes 2622976 | tf_op jit(solution)/shard_map/dot_general | solution.py:47
  37.6 0.3 collective-permute-start.5
  37.9 5.0 %collective-permute-start.6 = (bf16[256,128]{1,0:T(8,128)(2,1)S(1)}, bf16[256,128]{1,0:T(8,128)(2,1)S(1)}, u32[]{:S(2)}, u32[]{:S(2)}) collective-permute-start(bf16[256,128]{1,0:T(8,128)(2,1)S(1)} %get-tuple-element.11), channel_id=1, source_target_pairs={{1,0},{2,1},{3,2},{4,3},{5,4},{6,5},{7,6},{8,7},{9,8},{10,9},{11,1... | collective-permute-start | bytes 196616 | tf_op jit(solution)/shard_map/ppermute | solution.py:39
  43.0 0.0 copy-done.2
  43.0 0.1 slice.47
  43.1 0.3 copy.32
  43.3 1.6 %collective-permute-done.5 = bf16[256,128]{1,0:T(8,128)(2,1)S(1)} collective-permute-done((bf16[256,128]{1,0:T(8,128)(2,1)S(1)}, bf16[256,128]{1,0:T(8,128)(2,1)S(1)}, u32[]{:S(2)}, u32[]{:S(2)}) %collective-permute-start.5) | collective-permute-done | bytes 65568 | tf_op jit(solution)/shard_map/ppermute | solution.py:37
  44.9 0.0 collective-permute-done.6
  45.0 0.1 copy.33
  45.1 0.1 copy.34
  45.2 1.6 %scatter_fusion = f32[256,768]{0,1:T(8,128)S(1)} fusion(f32[256,768]{0,1:T(8,128)S(1)} %copy.32, s32[128]{0:T(128)S(1)} %get-tuple-element.19, f32[128,256]{1,0:T(8,128)S(1)} %copy.33), kind=kCustom, calls=%fused_computation.3 | custom fusion | flops 32768 | bytes 393728 | tf_op jit(solution)/shard_map/scatter-add | solution.py:123
  46.8 1.6 %scatter_fusion.1 = f32[256,768]{0,1:T(8,128)S(1)} fusion(f32[256,768]{0,1:T(8,128)S(1)} %scatter_fusion, s32[128]{0:T(128)S(1)} %get-tuple-element.18, f32[128,256]{1,0:T(8,128)S(1)} %copy.34), kind=kCustom, calls=%fused_computation.4 | custom fusion | flops 32768 | bytes 393728 | tf_op jit(solution)/shard_map/scatter-add | solution.py:124
  48.4 1.1 %copy.35 = f32[256,768]{1,0:T(8,128)} copy(f32[256,768]{0,1:T(8,128)S(1)} %scatter_fusion.1) | data formatting | bytes 1572864 | tf_op jit(solution)/shard_map/scatter-add | solution.py:124
  (17 shorter events, 0.2 us)
Async XLA Ops:
  0.0 12.4 %copy-start = (bf16[1024,384]{1,0:T(8,128)(2,1)S(1)}, bf16[1024,384]{1,0:T(8,128)(2,1)}, u32[]{:S(2)}) copy-start(bf16[1024,384]{1,0:T(8,128)(2,1)} %param.9) | copy-start | bytes 2359300
  0.0 10.5 %copy-start.1 = (s32[384,1]{0,1:T(1,128)S(1)}, s32[384,1]{0,1:T(1,128)}, u32[]{:S(2)}) copy-start(s32[384,1]{0,1:T(1,128)} %param.12) | copy-start | bytes 4612
  3.1 9.3 %collective-permute-start = (bf16[256,128]{0,1:T(8,128)(2,1)S(1)}, bf16[256,128]{0,1:T(8,128)(2,1)S(1)}, u32[]{:S(2)}, u32[]{:S(2)}) collective-permute-start(bf16[256,128]{0,1:T(8,128)(2,1)S(1)} %select_bitcast_fusion.1), channel_id=1, source_target_pairs={{0,1},{1,2},{2,3},{3,4},{4,5},{5,6},{6,7},{7,8},{8,9},{9,10},{10,1... | collective-permute-start | bytes 196616 | tf_op jit(solution)/shard_map/ppermute | solution.py:37
  4.5 7.9 %collective-permute-start.1 = (bf16[256,128]{0,1:T(8,128)(2,1)S(1)}, bf16[256,128]{0,1:T(8,128)(2,1)S(1)}, u32[]{:S(2)}, u32[]{:S(2)}) collective-permute-start(bf16[256,128]{0,1:T(8,128)(2,1)S(1)} %select_bitcast_fusion), channel_id=1, source_target_pairs={{1,0},{2,1},{3,2},{4,3},{5,4},{6,5},{7,6},{8,7},{9,8},{10,9},{11,1... | collective-permute-start | bytes 196616 | tf_op jit(solution)/shard_map/ppermute | solution.py:39
  12.3 5.0 %copy-start.3 = (s32[2,3]{1,0:T(2,128)S(1)}, s32[2,3]{1,0:T(2,128)}, u32[]{:S(2)}) copy-start(s32[2,3]{1,0:T(2,128)} %param.11) | copy-start | bytes 76
  13.9 9.4 %all-to-all-start = ((bf16[256,4,128]{2,0,1:T(8,128)(2,1)}), bf16[256,4,128]{2,0,1:T(8,128)(2,1)S(1)}, u32[]{:S(2)}, u32[]{:S(2)}) async-start(bf16[256,4,128]{2,0,1:T(8,128)(2,1)} %bitcast.103), calls=%async_computation | async-start | bytes 524288 | tf_op jit(solution)/shard_map/all_to_all | solution.py:105
  30.4 2.1 %collective-permute-start.2 = (bf16[256,128]{1,0:T(8,128)(2,1)S(1)}, bf16[256,128]{1,0:T(8,128)(2,1)S(1)}, u32[]{:S(2)}, u32[]{:S(2)}) collective-permute-start(bf16[256,128]{1,0:T(8,128)(2,1)S(1)} %bitcast.112), channel_id=1, source_target_pairs={{0,1},{1,0},{2,3},{3,2},{4,5},{5,4},{6,7},{7,6},{8,9},{9,8},{10,11... | collective-permute-start | bytes 196616 | tf_op jit(solution)/shard_map/ppermute | solution.py:25
  30.5 5.0 %collective-permute-start.3 = (bf16[256,128]{1,0:T(8,128)(2,1)S(1)}, bf16[256,128]{1,0:T(8,128)(2,1)S(1)}, u32[]{:S(2)}, u32[]{:S(2)}) collective-permute-start(bf16[256,128]{1,0:T(8,128)(2,1)S(1)} %bitcast.113), channel_id=1, source_target_pairs={{0,2},{1,3},{2,0},{3,1},{4,6},{5,7},{6,4},{7,5},{8,10},{9,11},{10,... | collective-permute-start | bytes 196616 | tf_op jit(solution)/shard_map/ppermute | solution.py:25
  31.0 5.0 %collective-permute-start.4 = (bf16[256,128]{1,0:T(8,128)(2,1)S(1)}, bf16[256,128]{1,0:T(8,128)(2,1)S(1)}, u32[]{:S(2)}, u32[]{:S(2)}) collective-permute-start(bf16[256,128]{1,0:T(8,128)(2,1)S(1)} %bitcast.114), channel_id=1, source_target_pairs={{0,3},{1,2},{2,1},{3,0},{4,7},{5,6},{6,5},{7,4},{8,11},{9,10},{10,... | collective-permute-start | bytes 196616 | tf_op jit(solution)/shard_map/ppermute | solution.py:25
  36.8 6.2 %copy-start.2 = (s32[2,128]{1,0:T(2,128)S(1)}, s32[2,128]{1,0:T(2,128)}, u32[]{:S(2)}) copy-start(s32[2,128]{1,0:T(2,128)} %param.13) | copy-start | bytes 3076
  37.6 7.3 %collective-permute-start.5 = (bf16[256,128]{1,0:T(8,128)(2,1)S(1)}, bf16[256,128]{1,0:T(8,128)(2,1)S(1)}, u32[]{:S(2)}, u32[]{:S(2)}) collective-permute-start(bf16[256,128]{1,0:T(8,128)(2,1)S(1)} %get-tuple-element.10), channel_id=1, source_target_pairs={{0,1},{1,2},{2,3},{3,4},{4,5},{5,6},{6,7},{7,8},{8,9},{9,10},{10,1... | collective-permute-start | bytes 196616 | tf_op jit(solution)/shard_map/ppermute | solution.py:37
  37.9 7.0 %collective-permute-start.6 = (bf16[256,128]{1,0:T(8,128)(2,1)S(1)}, bf16[256,128]{1,0:T(8,128)(2,1)S(1)}, u32[]{:S(2)}, u32[]{:S(2)}) collective-permute-start(bf16[256,128]{1,0:T(8,128)(2,1)S(1)} %get-tuple-element.11), channel_id=1, source_target_pairs={{1,0},{2,1},{3,2},{4,3},{5,4},{6,5},{7,6},{8,7},{9,8},{10,9},{11,1... | collective-permute-start | bytes 196616 | tf_op jit(solution)/shard_map/ppermute | solution.py:39
